TPU v7x, 128 devices: a whole 4x4x4 slice. The times are simulated.
128 devices in a mesh: ctx: 16 (over z, x), tp: 8 (over y, core).
Axes of the slice: x: 4, y: 4, z: 4, core: 2. Of those that a mesh axis runs over, the one named last changes fastest.
Arguments:
- hidden_in: bfloat16 [8192, 5376], P(('ctx', 'tp')), may hold values from -6 to 6
- stretch_start: int32 [1], replicated, may hold values from 1 to 1024
- pre_gain: float32 [5376], replicated, may hold values from 0.1 to 1.9
- q_weight: bfloat16 [5376, 4096], P('ctx', 'tp'), may hold values from -1 to 1
- k_weight: bfloat16 [5376, 2048], P('ctx', 'tp'), may hold values from -1 to 1
- v_weight: bfloat16 [5376, 2048], P('ctx', 'tp'), may hold values from -0.078125 to 0.078125
- o_weight: bfloat16 [4096, 5376], P('tp', 'ctx'), may hold values from -0.09375 to 0.09375
- q_gain: float32 [128], replicated, may hold values from 0.5 to 5
- k_gain: float32 [128], replicated, may hold values from 0.5 to 5
- prior_keys: bfloat16 [1024, 2048], P(None, 'tp'), may hold values from -6 to 6
- prior_values: bfloat16 [1024, 2048], P(None, 'tp'), may hold values from -6 to 6
- post_gain: float32 [5376], replicated, may hold values from 0.1 to 1.9
Outputs:
- result: bfloat16 [8192, 5376], P(('ctx', 'tp'))
All inputs are finite; a program needn't handle non-finite values.
Results may differ from a plain program's by a relative error of at most 0.013.
Values may be sent and summed in bfloat16 or wider, within the bound.
A program may use at most 128 MiB of HBM per device.

v0:
```python
import jax
import jax.numpy as jnp
from jax import lax
from jax.sharding import PartitionSpec as P

HD = 128
WINDOW = 1024
EPSILON = 1e-06
QUERY_FACTOR = 168.0 ** (-0.5)


def in_one_piece(arrays, axis, dim, along):
    ends, at = ([], 0)
    for a in arrays[:-1]:
        at += a.shape[along]
        ends.append(at)
    both = jnp.concatenate(arrays, axis=along)
    return tuple(jnp.split(lax.all_gather(both, axis, axis=dim, tiled=True), ends, axis=along))


def from_behind(value, axis, steps):
    count = lax.axis_size(axis)
    leading, last = (max(0, -steps), min(count, count - steps))
    return lax.ppermute(value, axis, [(source, source + steps) for source in range(leading, last)])


def rms_scale(inputs, scales):
    mean_sq = jnp.mean(inputs * inputs, axis=-1, keepdims=True)
    return inputs * lax.rsqrt(mean_sq + EPSILON) * scales


def rotate(inputs, positions):
    half_dim = inputs.shape[-1] // 2
    frequency = 10000.0 ** (-jnp.arange(half_dim, dtype=jnp.float32) / half_dim)
    angles = positions.astype(jnp.float32)[:, None] * frequency[None, :]
    cosines = jnp.cos(angles)[:, None, :]
    sines = jnp.sin(angles)[:, None, :]
    front = inputs[..., :half_dim]
    second = inputs[..., half_dim:]
    return jnp.concatenate(
        [front * cosines - second * sines, second * cosines + front * sines], axis=-1
    )


def local(
    hidden_in,
    stretch_start,
    pre_gain,
    q_weight,
    k_weight,
    v_weight,
    o_weight,
    q_gain,
    k_gain,
    prior_keys,
    prior_values,
    post_gain,
):
    residual_in = hidden_in.astype(jnp.float32)
    normed = rms_scale(residual_in, pre_gain).astype(jnp.bfloat16)
    block_rows = lax.all_gather(normed, "tp", axis=0, tiled=True)
    row_count = block_rows.shape[0]
    query_cols = q_weight.shape[1]
    kv_cols = k_weight.shape[1]

    def add_piece(segment):
        return jnp.dot(block_rows, segment, preferred_element_type=jnp.float32)

    segments = in_one_piece((q_weight, k_weight, v_weight), "ctx", 0, 1)
    query_raw, key_raw, value_raw = tuple((add_piece(segment) for segment in segments))
    local_heads = query_cols // HD
    local_kv = kv_cols // HD
    group = local_heads // local_kv
    chain_pos = lax.axis_index("ctx")
    positions = WINDOW + chain_pos * row_count + jnp.arange(row_count, dtype=jnp.int32)
    query = (
        rotate(rms_scale(query_raw.reshape(row_count, local_heads, HD), q_gain), positions)
        * QUERY_FACTOR
    ).astype(jnp.bfloat16)
    key_rows = (
        rotate(rms_scale(key_raw.reshape(row_count, local_kv, HD), k_gain), positions)
        .astype(jnp.bfloat16)
        .reshape(row_count, kv_cols)
    )
    value_rows = value_raw.astype(jnp.bfloat16)
    reach = WINDOW // row_count
    earlier = []
    current = (key_rows, value_rows)
    for hop_index in range(reach):
        current = from_behind((current[0], current[1]), "ctx", 1)
        earlier.append(current)
    key_parts = []
    value_parts = []
    for hop_index in range(reach - 1, -1, -1):
        source = chain_pos - (hop_index + 1)
        offset = jnp.maximum(WINDOW + source * row_count, 0)
        cached_keys = lax.dynamic_slice_in_dim(prior_keys, offset, row_count, 0)
        cached_values = lax.dynamic_slice_in_dim(prior_values, offset, row_count, 0)
        key_parts.append(jnp.where(source < 0, cached_keys, earlier[hop_index][0]))
        value_parts.append(jnp.where(source < 0, cached_values, earlier[hop_index][1]))
    key_parts.append(key_rows)
    value_parts.append(value_rows)
    span = (reach + 1) * row_count
    all_keys = jnp.concatenate(key_parts, axis=0).reshape(span, local_kv, HD)
    all_values = jnp.concatenate(value_parts, axis=0).reshape(span, local_kv, HD)
    key_anchor = WINDOW + (chain_pos - reach) * row_count
    query_grouped = query.reshape(row_count, local_kv, group, HD)
    scores = jnp.einsum(
        "qhgd,khd->hgqk", query_grouped, all_keys, preferred_element_type=jnp.float32
    )
    key_pos = key_anchor + jnp.arange(span, dtype=jnp.int32)
    first_valid = WINDOW - stretch_start[0]
    allowed = (
        (key_pos[None, :] <= positions[:, None])
        & (key_pos[None, :] > positions[:, None] - WINDOW)
        & (key_pos[None, :] >= first_valid)
    )
    scores = jnp.where(allowed[None, None, :, :], scores, jnp.float32(-1e30))
    largest = jnp.max(scores, axis=-1, keepdims=True)
    expon = jnp.exp(scores - largest)
    attn_probs = (expon / jnp.sum(expon, axis=-1, keepdims=True)).astype(jnp.bfloat16)
    attended = jnp.einsum(
        "hgqk,khd->qhgd", attn_probs, all_values, preferred_element_type=jnp.float32
    )
    attended = attended.astype(jnp.bfloat16).reshape(row_count, query_cols)
    partial_rows = jnp.dot(
        attended,
        lax.all_gather(o_weight, "ctx", axis=1, tiled=True),
        preferred_element_type=jnp.float32,
    )
    summed = lax.psum_scatter(
        partial_rows.astype(jnp.bfloat16), "tp", scatter_dimension=0, tiled=True
    ).astype(jnp.float32)
    return (residual_in + rms_scale(summed, post_gain)).astype(jnp.bfloat16)


def solution(mesh):
    return jax.shard_map(
        local,
        mesh=mesh,
        in_specs=(
            P(("ctx", "tp"), None),
            P(),
            P(),
            P("ctx", "tp"),
            P("ctx", "tp"),
            P("ctx", "tp"),
            P("tp", "ctx"),
            P(),
            P(),
            P(None, "tp"),
            P(None, "tp"),
            P(),
        ),
        out_specs=P(("ctx", "tp"), None),
        check_vma=False,
    )
```

profile of v0, /device:TPU:0, one launch (start us, length us, event | category | flops | bytes accessed | tf_op | source)
XLA Modules:
  0.0 256.0 jit_solution(17121036638809811373)
XLA Ops:
  6.5 1.3 fusion.15
  7.9 2.2 fusion.17
  10.1 2.1 pad_maximum_fusion.1
  14.6 1.9 and_and_fusion
  16.5 33.8 %all-gather.4.cloned.1.call-done = bf16[512,5376]{1,0:T(8,128)(2,1)} async-done(((bf16[64,5376]{1,0:T(8,128)(2,1)}), bf16[512,5376]{1,0:T(8,128)(2,1)}) %all-gather.4.cloned.1.call-update) | async-done | bytes 5505040 | tf_op jit(solution)/shard_map/all_gather | solution.py:61
  50.3 85.0 %all-gather.6.cloned.1.call-done = bf16[5376,1024]{1,0:T(8,128)(2,1)} async-done(((bf16[336,1024]{1,0:T(8,128)(2,1)}), bf16[5376,1024]{1,0:T(8,128)(2,1)}) %all-gather.6.cloned.1.call-update) | async-done | bytes 11010064 | tf_op jit(solution)/shard_map/all_gather | solution.py:18
  135.3 5.1 %fusion.20 = bf16[512,256]{1,0:T(8,128)(2,1)S(1)} fusion(bf16[512,5376]{1,0:T(8,128)(2,1)} %all-gather.4.cloned.1.call-done, bf16[5376,1024]{1,0:T(8,128)(2,1)} %all-gather.6.cloned.1.call-done), kind=kOutput, calls=%fused_computation.29 | convolution fusion | flops 1409417216 | bytes 8519680 | tf_op jit(solution)/shard_map/dot_general | solution.py:67
  140.4 4.2 %collective-permute-start = (bf16[512,256]{1,0:T(8,128)(2,1)S(1)}, bf16[512,256]{1,0:T(8,128)(2,1)}, u32[]{:S(2)}, u32[]{:S(2)}) collective-permute-start(bf16[512,256]{1,0:T(8,128)(2,1)S(1)} %fusion.20), channel_id=1, source_target_pairs={{0,8},{8,16},{16,24},{24,32},{32,40},{40,48},{48,56},{56,64},{64,7... | collective-permute-start | bytes 786440 | tf_op jit(solution)/shard_map/ppermute | solution.py:24
  144.6 3.5 %multiply_reduce_fusion.1 = (f32[512,2]{0,1:T(2,128)S(1)}, f32[512,256]{0,1:T(8,128)S(1)}) fusion(bf16[512,5376]{1,0:T(8,128)(2,1)S(1)} %copy-done.7, bf16[5376,1024]{1,0:T(8,128)(2,1)} %all-gather.6.cloned.1.call-done), kind=kOutput, calls=%fused_computation.43 | convolution fusion | flops 1409547264 | bytes 8785920 | tf_op jit(solution)/shard_map/dot_general | solution.py:67
  149.7 3.5 %collective-permute-start.2 = (bf16[512,256]{1,0:T(8,128)(2,1)}, bf16[512,256]{1,0:T(8,128)(2,1)}, u32[]{:S(2)}, u32[]{:S(2)}) collective-permute-start(bf16[512,256]{1,0:T(8,128)(2,1)} %copy_bitcast_fusion), channel_id=1, source_target_pairs={{0,8},{8,16},{16,24},{24,32},{32,40},{40,48},{48,56},{56,64},{64,7... | collective-permute-start | bytes 786440 | tf_op jit(solution)/shard_map/ppermute | solution.py:24
  153.2 6.8 %multiply_reduce_fusion = (f32[512,4]{0,1:T(4,128)S(1)}, f32[512,512]{0,1:T(8,128)S(1)}) fusion(bf16[512,5376]{1,0:T(8,128)(2,1)} %all-gather.4.cloned.1.call-done, bf16[5376,1024]{1,0:T(8,128)(2,1)} %all-gather.6.cloned.1.call-done), kind=kOutput, calls=%fused_computation.33 | convolution fusion | flops 2819094528 | bytes 12066816 | tf_op jit(solution)/shard_map/dot_general | solution.py:67
  160.2 3.1 %collective-permute-start.1 = (bf16[512,256]{1,0:T(8,128)(2,1)}, bf16[512,256]{1,0:T(8,128)(2,1)}, u32[]{:S(2)}, u32[]{:S(2)}) collective-permute-start(bf16[512,256]{1,0:T(8,128)(2,1)} %collective-permute-done), channel_id=1, source_target_pairs={{0,8},{8,16},{16,24},{24,32},{32,40},{40,48},{48,56},{56,64},{64,7... | collective-permute-start | bytes 786440 | tf_op jit(solution)/shard_map/ppermute | solution.py:24
  165.1 3.2 %collective-permute-start.3 = (bf16[512,256]{1,0:T(8,128)(2,1)}, bf16[512,256]{1,0:T(8,128)(2,1)}, u32[]{:S(2)}, u32[]{:S(2)}) collective-permute-start(bf16[512,256]{1,0:T(8,128)(2,1)} %collective-permute-done.2), channel_id=1, source_target_pairs={{0,8},{8,16},{16,24},{24,32},{32,40},{40,48},{48,56},{56,64},{64,7... | collective-permute-start | bytes 786440 | tf_op jit(solution)/shard_map/ppermute | solution.py:24
  168.7 1.2 dynamic-slice_select_fusion.1
  170.0 1.1 pad_maximum_fusion
  171.0 1.2 copy.36
  172.2 5.2 %collective-permute-done.3 = bf16[512,256]{1,0:T(8,128)(2,1)} collective-permute-done((bf16[512,256]{1,0:T(8,128)(2,1)}, bf16[512,256]{1,0:T(8,128)(2,1)}, u32[]{:S(2)}, u32[]{:S(2)}) %collective-permute-start.3) | collective-permute-done | bytes 262176 | tf_op jit(solution)/shard_map/ppermute | solution.py:24
  177.7 10.2 %fusion.32 = (f32[2,2,512]{2,1,0:T(2,128)S(1)}, f32[2,2,512,1536]{2,3,1,0:T(8,128)}) fusion(pred[512,1536]{0,1:T(8,128)(4,1)} %and_and_fusion, bf16[512,2,128]{2,0,1:T(8,128)(2,1)} %maximum_convert_fusion, bf16[512,2,128]{2,0,1:T(8,128)(2,1)S(1)} %get-tuple-element.23, bf16[512,2,128]{2,0,1:T(8,128)(2,1)S(1)} %get-tuple-element.24, ...), kind=kOutput, calls=%fused_computation.67 | convolution fusion | flops 817890816 | bytes 15212544 | tf_op jit(solution)/shard_map/sub | solution.py:120
  187.9 5.8 %fusion.19 = bf16[2,128,2,512]{3,1,2,0:T(8,128)(2,1)S(1)} fusion(bf16[1536,2,128,1]{0,2,3,1:T(8,128)(2,1)S(1)} %bitcast.62, f32[2,2,512,1536]{2,3,1,0:T(8,128)} %get-tuple-element.20, f32[2,2,512]{2,1,0:T(2,128)S(1)} %get-tuple-element.19), kind=kOutput, calls=%fused_computation.28 | convolution fusion | flops 811859968 | bytes 13901824 | tf_op jit(solution)/shard_map/hgqk,khd->qhgd/dot_general | solution.py:122
  193.7 4.2 %all-gather.8.cloned.1.call-done = bf16[512,5376]{0,1:T(8,128)(2,1)} async-done(((bf16[512,336]{0,1:T(8,128)(2,1)}), bf16[512,5376]{0,1:T(8,128)(2,1)}) %all-gather.8.cloned.1.call-update) | async-done | bytes 5505040 | tf_op jit(solution)/shard_map/all_gather | solution.py:128
  197.9 7.5 %convolution_convert_fusion = bf16[512,5376]{1,0:T(8,128)(2,1)} fusion(bf16[512,512]{0,1:T(8,128)(2,1)S(1)} %bitcast.64, bf16[512,5376]{0,1:T(8,128)(2,1)} %all-gather.8.cloned.1.call-done), kind=kOutput, calls=%fused_computation.5 | convolution fusion | flops 2821324800 | bytes 11534336 | tf_op jit(solution)/shard_map/dot_general | solution.py:126
  205.5 40.4 %reduce-scatter.2.cloned.1.call-done = bf16[64,5376]{1,0:T(8,128)(2,1)} async-done(((bf16[512,5376]{1,0:T(8,128)(2,1)}), bf16[64,5376]{1,0:T(8,128)(2,1)}) %reduce-scatter.2.cloned.1.call-update) | async-done | bytes 688144 | tf_op jit(solution)/shard_map/reduce_scatter | solution.py:131
  245.8 1.3 fusion.13
  247.2 2.3 fusion.18
  (50 shorter events, 5.9 us)
Async XLA Ops:
  6.5 43.8 %all-gather.4.cloned.1.call-start = ((), (), s32[]{:S(2)}) async-start(), calls=%async_computation.1 | async-start | bytes 6193152 | tf_op jit(solution)/shard_map/all_gather | solution.py:61
  10.1 125.2 %all-gather.6.cloned.1.call-start = ((), (), s32[]{:S(2)}) async-start(), calls=%async_computation.2 | async-start | bytes 11698176 | tf_op jit(solution)/shard_map/all_gather | solution.py:18
  12.3 185.7 %all-gather.8.cloned.1.call-start = ((), (), s32[]{:S(2)}) async-start(), calls=%async_computation.3 | async-start | bytes 5849088 | tf_op jit(solution)/shard_map/all_gather | solution.py:128
  13.0 232.8 %reduce-scatter.2.cloned.1.call-start = ((), (), s32[]{:S(2)}) async-start(), calls=%async_computation.4 | async-start | bytes 6193152 | tf_op jit(solution)/shard_map/reduce_scatter | solution.py:131
  135.3 9.4 %copy-start.7 = (bf16[512,5376]{1,0:T(8,128)(2,1)S(1)}, bf16[512,5376]{1,0:T(8,128)(2,1)}, u32[]{:S(2)}) copy-start(bf16[512,5376]{1,0:T(8,128)(2,1)} %all-gather.4.cloned.1.call-done) | copy-start | bytes 16515076
  140.4 7.9 %copy-start.3 = (bf16[512,256]{1,0:T(8,128)(2,1)}, bf16[512,256]{1,0:T(8,128)(2,1)S(1)}, u32[]{:S(2)}) copy-start(bf16[512,256]{1,0:T(8,128)(2,1)S(1)} %fusion.20) | copy-start | bytes 786436
  140.4 7.9 %copy-start.5 = (f32[128]{0:T(128)S(1)}, f32[128]{0:T(128)}, u32[]{:S(2)}) copy-start(f32[128]{0:T(128)} %param.20) | copy-start | bytes 1540
  140.4 19.8 %collective-permute-start = (bf16[512,256]{1,0:T(8,128)(2,1)S(1)}, bf16[512,256]{1,0:T(8,128)(2,1)}, u32[]{:S(2)}, u32[]{:S(2)}) collective-permute-start(bf16[512,256]{1,0:T(8,128)(2,1)S(1)} %fusion.20), channel_id=1, source_target_pairs={{0,8},{8,16},{16,24},{24,32},{32,40},{40,48},{48,56},{56,64},{64,7... | collective-permute-start | bytes 786440 | tf_op jit(solution)/shard_map/ppermute | solution.py:24
  149.7 10.3 %copy-start.6 = (f32[128]{0:T(128)S(1)}, f32[128]{0:T(128)}, u32[]{:S(2)}) copy-start(f32[128]{0:T(128)} %param.19) | copy-start | bytes 1540
  149.7 15.4 %collective-permute-start.2 = (bf16[512,256]{1,0:T(8,128)(2,1)}, bf16[512,256]{1,0:T(8,128)(2,1)}, u32[]{:S(2)}, u32[]{:S(2)}) collective-permute-start(bf16[512,256]{1,0:T(8,128)(2,1)} %copy_bitcast_fusion), channel_id=1, source_target_pairs={{0,8},{8,16},{16,24},{24,32},{32,40},{40,48},{48,56},{56,64},{64,7... | collective-permute-start | bytes 786440 | tf_op jit(solution)/shard_map/ppermute | solution.py:24
  160.2 8.5 %collective-permute-start.1 = (bf16[512,256]{1,0:T(8,128)(2,1)}, bf16[512,256]{1,0:T(8,128)(2,1)}, u32[]{:S(2)}, u32[]{:S(2)}) collective-permute-start(bf16[512,256]{1,0:T(8,128)(2,1)} %collective-permute-done), channel_id=1, source_target_pairs={{0,8},{8,16},{16,24},{24,32},{32,40},{40,48},{48,56},{56,64},{64,7... | collective-permute-start | bytes 786440 | tf_op jit(solution)/shard_map/ppermute | solution.py:24
  164.2 13.2 %copy-start.2 = (bf16[1024,256]{1,0:T(8,128)(2,1)S(1)}, bf16[1024,256]{1,0:T(8,128)(2,1)}, u32[]{:S(2)}) copy-start(bf16[1024,256]{1,0:T(8,128)(2,1)} %param.21) | copy-start | bytes 1572868
  165.1 12.3 %collective-permute-start.3 = (bf16[512,256]{1,0:T(8,128)(2,1)}, bf16[512,256]{1,0:T(8,128)(2,1)}, u32[]{:S(2)}, u32[]{:S(2)}) collective-permute-start(bf16[512,256]{1,0:T(8,128)(2,1)} %collective-permute-done.2), channel_id=1, source_target_pairs={{0,8},{8,16},{16,24},{24,32},{32,40},{40,48},{48,56},{56,64},{64,7... | collective-permute-start | bytes 786440 | tf_op jit(solution)/shard_map/ppermute | solution.py:24
  177.7 10.2 %copy-start.1 = (bf16[1536,256]{0,1:T(8,128)(2,1)S(1)}, bf16[1536,256]{0,1:T(8,128)(2,1)}, u32[]{:S(2)}) copy-start(bf16[1536,256]{0,1:T(8,128)(2,1)} %copy.36) | copy-start | bytes 2359300
  205.5 41.7 %copy-start = (bf16[64,5376]{1,0:T(8,128)(2,1)S(1)}, bf16[64,5376]{1,0:T(8,128)(2,1)}, u32[]{:S(2)}) copy-start(bf16[64,5376]{1,0:T(8,128)(2,1)} %param.12) | copy-start | bytes 2064388
  205.5 41.7 %copy-start.4 = (f32[5376]{0:T(1024)S(1)}, f32[5376]{0:T(1024)}, u32[]{:S(2)}) copy-start(f32[5376]{0:T(1024)} %param.23) | copy-start | bytes 64516
Sparse Core Ops, SparseCore 0:
  10.2 40.0 all-gather.3
  52.4 82.7 all-gather.5
  137.4 60.4 all-gather.7
  205.6 40.1 reduce-scatter.1
where the time goes:
time: 257 us; the launch traced here: 256 us
  waiting for transfers between devices  170 us (66%)
  matrix products  38.9 us (15%)
  other arithmetic  16.7 us (6%)
  starting transfers between devices  14.1 us (5%)
  between operations  14 us (5%)
    all_gather x1, waiting for transfers between devices, in_one_piece(): lax.all_gather(both, axis, axis=dim, tiled=True)  85 us
    reduce_scatter x1, waiting for transfers between devices, local(): lax.psum_scatter(partial_rows.astype(jnp.bfloat16), 'tp', scatter_dimensi...  40.4 us
    all_gather x1, waiting for transfers between devices, local(): block_rows = lax.all_gather(normed, 'tp', axis=0, tiled=True)  33.8 us
    dot_general x3, matrix products, add_piece(): return jnp.dot(block_rows, segment, preferred_element_type=jnp.float32)  15.4 us
    ppermute x4, starting transfers between devices, from_behind(): lax.ppermute(value, axis, [(source, source + steps) for source in range(l...  14 us
    sub x1, matrix products, local(): expon = jnp.exp(scores - largest)  10.2 us
    dot_general x1, matrix products, local(): jnp.dot(attended, lax.all_gather(o_weight, 'ctx', axis=1, tiled=True), pr...  7.51 us
    dot_general x1, matrix products, local(): jnp.einsum('hgqk,khd->qhgd', attn_probs, all_values, preferred_element_ty...  5.77 us
  transfers between devices with their start and end apart: 8, of which 6 were waited for; matrix products, arithmetic and copies ran while one was open for 17% of the time, Pallas kernels for 0%

commit v1 on v0

--- a/solution.py
+++ b/solution.py
@@ -1,12 +1,33 @@
+import functools
 import jax
 import jax.numpy as jnp
 from jax import lax
 from jax.sharding import PartitionSpec as P
+from jax.lax import axis_index, axis_size, ppermute
 
 HD = 128
 WINDOW = 1024
 EPSILON = 1e-06
 QUERY_FACTOR = 168.0 ** (-0.5)
+
+
+def manage_routes_all(unit, k_dim):
+    n_lanes = axis_size("tp")
+    pieces_in = [unit]
+    for s in range(n_lanes - 1):
+        next_value = ppermute(
+            pieces_in[-1],
+            axis_name="tp",
+            perm=[(dev_i, (dev_i + 1) % n_lanes) for dev_i in range(n_lanes)],
+        )
+        pieces_in.append(next_value)
+    y = jnp.concatenate(pieces_in[::-1], axis=k_dim)
+    kept_arr = axis_index("tp")
+    state_next = jnp.roll(y, (kept_arr + 1) * unit.shape[k_dim], axis=k_dim)
+    return state_next
+
+
+steps_all_open = functools.partial(manage_routes_all, k_dim=0)
 
 
 def in_one_piece(arrays, axis, dim, along):
@@ -58,7 +79,7 @@
 ):
     residual_in = hidden_in.astype(jnp.float32)
     normed = rms_scale(residual_in, pre_gain).astype(jnp.bfloat16)
-    block_rows = lax.all_gather(normed, "tp", axis=0, tiled=True)
+    block_rows = steps_all_open(normed)
     row_count = block_rows.shape[0]
     query_cols = q_weight.shape[1]
     kv_cols = k_weight.shape[1]

time: 257 us -> 241 us (0.938)
  waiting for transfers between devices: 170 us -> 128 us
  local copies, waits for them, and re-layouts: 2.41 us -> 22.9 us
  other arithmetic: 16.7 us -> 19.7 us
    all_gather x1, waiting for transfers between devices: 85 us -> 0.01 us  [in_one_piece(): lax.all_gather(both, axis, axis=dim, tiled=True)]
    ppermute x0 -> x7, waiting for transfers between devices: none -> 74.2 us  [manage_routes_all(): ppermute(pieces_in[-1], axis_name='tp', perm=[(dev_i, (dev_i + 1) % n_lan...]
    all_gather x1 -> x0, waiting for transfers between devices: 33.8 us -> none  [local(): block_rows = lax.all_gather(normed, 'tp', axis=0, tiled=True)]
    unnamed x16 -> x34, local copies, waits for them, and re-layouts: 0.04 us -> 17.2 us
    ppermute x4, waiting for transfers between devices: 5.67 us -> 12 us  [from_behind(): lax.ppermute(value, axis, [(source, source + steps) for source in range(l...]
    all_gather x1, waiting for transfers between devices: 4.23 us -> 0.02 us  [local(): lax.all_gather(o_weight, 'ctx', axis=1, tiled=True)]
  transfers between devices with their start and end apart: 8 -> 14, of which waited for: 6 -> 10; matrix products, arithmetic and copies ran while one was open for 17% -> 29% of each run, Pallas kernels for 0% -> 0%
where the time goes in v1:
time: 241 us; the launch traced here: 240 us
  waiting for transfers between devices  128 us (53%)
  matrix products  40.4 us (17%)
  local copies, waits for them, and re-layouts  22.9 us (10%)
  other arithmetic  19.7 us (8%)
  starting transfers between devices  15.1 us (6%)
  between operations  14.1 us (6%)
    ppermute x7, waiting for transfers between devices, manage_routes_all(): ppermute(pieces_in[-1], axis_name='tp', perm=[(dev_i, (dev_i + 1) % n_lan...  74.2 us
    reduce_scatter x1, waiting for transfers between devices, local(): lax.psum_scatter(partial_rows.astype(jnp.bfloat16), 'tp', scatter_dimensi...  41.5 us
    unnamed x34, local copies, waits for them, and re-layouts  17.2 us
    dot_general x3, matrix products, add_piece(): return jnp.dot(block_rows, segment, preferred_element_type=jnp.float32)  16.9 us
    ppermute x4, starting transfers between devices, from_behind(): lax.ppermute(value, axis, [(source, source + steps) for source in range(l...  15 us
    ppermute x4, waiting for transfers between devices, from_behind(): lax.ppermute(value, axis, [(source, source + steps) for source in range(l...  12 us
    sub x1, matrix products, local(): expon = jnp.exp(scores - largest)  10.4 us
    dot_general x1, matrix products, local(): jnp.dot(attended, lax.all_gather(o_weight, 'ctx', axis=1, tiled=True), pr...  7.51 us
  transfers between devices with their start and end apart: 14, of which 10 were waited for; matrix products, arithmetic and copies ran while one was open for 29% of the time, Pallas kernels for 0%

profile of v1, /device:TPU:0, one launch (start us, length us, event | category | flops | bytes accessed | tf_op | source)
XLA Modules:
  0.0 240.0 jit_solution(1282670732980351935)
XLA Ops:
  6.5 2.1 pad_maximum_fusion.1
  11.5 11.6 %collective-permute-done = bf16[64,5376]{1,0:T(8,128)(2,1)S(1)} collective-permute-done((bf16[64,5376]{1,0:T(8,128)(2,1)S(1)}, bf16[64,5376]{1,0:T(8,128)(2,1)S(1)}, u32[]{:S(2)}, u32[]{:S(2)}) %collective-permute-start) | collective-permute-done | bytes 688160 | tf_op jit(solution)/shard_map/ppermute | solution.py:18
  23.0 11.6 %collective-permute-done.1 = bf16[64,5376]{1,0:T(8,128)(2,1)S(1)} collective-permute-done((bf16[64,5376]{1,0:T(8,128)(2,1)S(1)}, bf16[64,5376]{1,0:T(8,128)(2,1)S(1)}, u32[]{:S(2)}, u32[]{:S(2)}) %collective-permute-start.1) | collective-permute-done | bytes 688160 | tf_op jit(solution)/shard_map/ppermute | solution.py:18
  34.6 11.6 %collective-permute-done.2 = bf16[64,5376]{1,0:T(8,128)(2,1)S(1)} collective-permute-done((bf16[64,5376]{1,0:T(8,128)(2,1)S(1)}, bf16[64,5376]{1,0:T(8,128)(2,1)S(1)}, u32[]{:S(2)}, u32[]{:S(2)}) %collective-permute-start.2) | collective-permute-done | bytes 688160 | tf_op jit(solution)/shard_map/ppermute | solution.py:18
  46.2 11.6 %collective-permute-done.3 = bf16[64,5376]{1,0:T(8,128)(2,1)S(1)} collective-permute-done((bf16[64,5376]{1,0:T(8,128)(2,1)S(1)}, bf16[64,5376]{1,0:T(8,128)(2,1)S(1)}, u32[]{:S(2)}, u32[]{:S(2)}) %collective-permute-start.3) | collective-permute-done | bytes 688160 | tf_op jit(solution)/shard_map/ppermute | solution.py:18
  57.8 11.7 %collective-permute-done.4 = bf16[64,5376]{1,0:T(8,128)(2,1)} collective-permute-done((bf16[64,5376]{1,0:T(8,128)(2,1)S(1)}, bf16[64,5376]{1,0:T(8,128)(2,1)}, u32[]{:S(2)}, u32[]{:S(2)}) %collective-permute-start.4) | collective-permute-done | bytes 688160 | tf_op jit(solution)/shard_map/ppermute | solution.py:18
  75.0 6.3 %collective-permute-done.5 = bf16[64,5376]{1,0:T(8,128)(2,1)} collective-permute-done((bf16[64,5376]{1,0:T(8,128)(2,1)}, bf16[64,5376]{1,0:T(8,128)(2,1)}, u32[]{:S(2)}, u32[]{:S(2)}) %collective-permute-start.5) | collective-permute-done | bytes 688160 | tf_op jit(solution)/shard_map/ppermute | solution.py:18
  83.2 9.9 %collective-permute-done.6 = bf16[64,5376]{1,0:T(8,128)(2,1)S(1)} collective-permute-done((bf16[64,5376]{1,0:T(8,128)(2,1)}, bf16[64,5376]{1,0:T(8,128)(2,1)S(1)}, u32[]{:S(2)}, u32[]{:S(2)}) %collective-permute-start.6) | collective-permute-done | bytes 688160 | tf_op jit(solution)/shard_map/ppermute | solution.py:18
  96.0 2.0 constant_dynamic-update-slice_fusion.13
  105.6 2.1 constant_dynamic-update-slice_fusion.5
  112.4 5.1 %fusion.23 = bf16[512,256]{1,0:T(8,128)(2,1)S(1)} fusion(bf16[5376,1024]{1,0:T(8,128)(2,1)} %all-gather.3.cloned.1.call-done, bf16[1024,5376]{1,0:T(8,128)(2,1)} %constant_dynamic-update-slice_fusion, s32[]{:T(128)S(6)} %select_n.45), kind=kOutput, calls=%fused_computation.32 | convolution fusion | flops 1409417216 | bytes 8519684 | tf_op jit(solution)/shard_map/dot_general | solution.py:88
  117.6 4.2 %collective-permute-start.7 = (bf16[512,256]{1,0:T(8,128)(2,1)S(1)}, bf16[512,256]{1,0:T(8,128)(2,1)}, u32[]{:S(2)}, u32[]{:S(2)}) collective-permute-start(bf16[512,256]{1,0:T(8,128)(2,1)S(1)} %fusion.23), channel_id=1, source_target_pairs={{0,8},{8,16},{16,24},{24,32},{32,40},{40,48},{48,56},{56,64},{64,7... | collective-permute-start | bytes 786440 | tf_op jit(solution)/shard_map/ppermute | solution.py:45
  121.8 5.1 %multiply_reduce_fusion.1 = (f32[512,2]{0,1:T(2,128)S(1)}, f32[512,256]{0,1:T(8,128)S(1)}) fusion(bf16[5376,1024]{1,0:T(8,128)(2,1)} %all-gather.3.cloned.1.call-done, bf16[1024,5376]{1,0:T(8,128)(2,1)} %constant_dynamic-update-slice_fusion, s32[]{:T(128)S(6)} %select_n.45), kind=kOutput, calls=%fused_computation.46 | convolution fusion | flops 1409547264 | bytes 8785924 | tf_op jit(solution)/shard_map/dot_general | solution.py:88
  128.4 3.5 %collective-permute-start.9 = (bf16[512,256]{1,0:T(8,128)(2,1)}, bf16[512,256]{1,0:T(8,128)(2,1)}, u32[]{:S(2)}, u32[]{:S(2)}) collective-permute-start(bf16[512,256]{1,0:T(8,128)(2,1)} %copy_bitcast_fusion), channel_id=1, source_target_pairs={{0,8},{8,16},{16,24},{24,32},{32,40},{40,48},{48,56},{56,64},{64,7... | collective-permute-start | bytes 786440 | tf_op jit(solution)/shard_map/ppermute | solution.py:45
  131.9 6.7 %multiply_reduce_fusion = (f32[512,4]{0,1:T(4,128)S(1)}, f32[512,512]{0,1:T(8,128)S(1)}) fusion(bf16[5376,1024]{1,0:T(8,128)(2,1)} %all-gather.3.cloned.1.call-done, bf16[1024,5376]{1,0:T(8,128)(2,1)} %constant_dynamic-update-slice_fusion, s32[]{:T(128)S(6)} %select_n.45), kind=kOutput, calls=%fused_computation.36 | convolution fusion | flops 2819094528 | bytes 12066820 | tf_op jit(solution)/shard_map/dot_general | solution.py:88
  138.9 3.1 %collective-permute-start.8 = (bf16[512,256]{1,0:T(8,128)(2,1)}, bf16[512,256]{1,0:T(8,128)(2,1)}, u32[]{:S(2)}, u32[]{:S(2)}) collective-permute-start(bf16[512,256]{1,0:T(8,128)(2,1)} %collective-permute-done.7), channel_id=1, source_target_pairs={{0,8},{8,16},{16,24},{24,32},{32,40},{40,48},{48,56},{56,64},{64,7... | collective-permute-start | bytes 786440 | tf_op jit(solution)/shard_map/ppermute | solution.py:45
  144.8 4.1 %collective-permute-start.10 = (bf16[512,256]{1,0:T(8,128)(2,1)}, bf16[512,256]{1,0:T(8,128)(2,1)}, u32[]{:S(2)}, u32[]{:S(2)}) collective-permute-start(bf16[512,256]{1,0:T(8,128)(2,1)} %collective-permute-done.9), channel_id=1, source_target_pairs={{0,8},{8,16},{16,24},{24,32},{32,40},{40,48},{48,56},{56,64},{64,7... | collective-permute-start | bytes 786440 | tf_op jit(solution)/shard_map/ppermute | solution.py:45
  148.9 6.1 %collective-permute-done.8 = bf16[512,256]{1,0:T(8,128)(2,1)} collective-permute-done((bf16[512,256]{1,0:T(8,128)(2,1)}, bf16[512,256]{1,0:T(8,128)(2,1)}, u32[]{:S(2)}, u32[]{:S(2)}) %collective-permute-start.8) | collective-permute-done | bytes 262176 | tf_op jit(solution)/shard_map/ppermute | solution.py:45
  157.5 5.9 %collective-permute-done.10 = bf16[512,256]{1,0:T(8,128)(2,1)} collective-permute-done((bf16[512,256]{1,0:T(8,128)(2,1)}, bf16[512,256]{1,0:T(8,128)(2,1)}, u32[]{:S(2)}, u32[]{:S(2)}) %collective-permute-start.10) | collective-permute-done | bytes 262176 | tf_op jit(solution)/shard_map/ppermute | solution.py:45
  164.7 10.4 %fusion.40 = (f32[2,2,512]{2,1,0:T(2,128)S(1)}, f32[2,2,512,1536]{2,3,1,0:T(8,128)}) fusion(pred[512,1536]{0,1:T(8,128)(4,1)} %and_and_fusion, bf16[512,2,128]{2,0,1:T(8,128)(2,1)} %maximum_convert_fusion, bf16[512,2,128]{2,0,1:T(8,128)(2,1)S(1)} %get-tuple-element.23, bf16[512,2,128]{2,0,1:T(8,128)(2,1)S(1)} %get-tuple-element.24, ...), kind=kOutput, calls=%fused_computation.89 | convolution fusion | flops 817890816 | bytes 15212544 | tf_op jit(solution)/shard_map/sub | solution.py:141
  175.2 5.6 %fusion.22 = bf16[2,128,2,512]{3,1,2,0:T(8,128)(2,1)S(1)} fusion(bf16[1536,2,128,1]{0,2,3,1:T(8,128)(2,1)S(1)} %bitcast.59, f32[2,2,512,1536]{2,3,1,0:T(8,128)} %get-tuple-element.20, f32[2,2,512]{2,1,0:T(2,128)S(1)} %get-tuple-element.19), kind=kOutput, calls=%fused_computation.31 | convolution fusion | flops 811859968 | bytes 13901824 | tf_op jit(solution)/shard_map/hgqk,khd->qhgd/dot_general | solution.py:143
  180.8 7.5 %convolution_convert_fusion = bf16[512,5376]{1,0:T(8,128)(2,1)} fusion(bf16[512,512]{0,1:T(8,128)(2,1)S(1)} %bitcast.61, bf16[512,5376]{0,1:T(8,128)(2,1)} %all-gather.5.cloned.1.call-done), kind=kOutput, calls=%fused_computation.5 | convolution fusion | flops 2821324800 | bytes 11534336 | tf_op jit(solution)/shard_map/dot_general | solution.py:147
  188.3 41.5 %reduce-scatter.2.cloned.1.call-done = bf16[64,5376]{1,0:T(8,128)(2,1)} async-done(((bf16[512,5376]{1,0:T(8,128)(2,1)}), bf16[64,5376]{1,0:T(8,128)(2,1)}) %reduce-scatter.2.cloned.1.call-update) | async-done | bytes 688144 | tf_op jit(solution)/shard_map/reduce_scatter | solution.py:152
  231.2 2.3 fusion.21
  (81 shorter events, 34.3 us)
Async XLA Ops:
  6.5 95.1 %copy-start = (bf16[64,5376]{1,0:T(8,128)(2,1)S(1)}, bf16[64,5376]{1,0:T(8,128)(2,1)}, u32[]{:S(2)}) copy-start(bf16[64,5376]{1,0:T(8,128)(2,1)} %param.12) | copy-start | bytes 2064388
  6.5 95.1 %copy-start.6 = (f32[5376]{0:T(1024)S(1)}, f32[5376]{0:T(1024)}, u32[]{:S(2)}) copy-start(f32[5376]{0:T(1024)} %param.14) | copy-start | bytes 64516
  6.5 105.9 %all-gather.3.cloned.1.call-start = ((), (), s32[]{:S(2)}) async-start(), calls=%async_computation.1 | async-start | bytes 11698176 | tf_op jit(solution)/shard_map/all_gather | solution.py:39
  8.7 172.1 %all-gather.5.cloned.1.call-start = ((), (), s32[]{:S(2)}) async-start(), calls=%async_computation.2 | async-start | bytes 5849088 | tf_op jit(solution)/shard_map/all_gather | solution.py:149
  11.5 11.6 %collective-permute-start = (bf16[64,5376]{1,0:T(8,128)(2,1)S(1)}, bf16[64,5376]{1,0:T(8,128)(2,1)S(1)}, u32[]{:S(2)}, u32[]{:S(2)}) collective-permute-start(bf16[64,5376]{1,0:T(8,128)(2,1)S(1)} %fusion.20), channel_id=1, source_target_pairs={{0,1},{1,2},{2,3},{3,4},{4,5},{5,6},{6,7},{7,0},{8,9},{9,10},{10,1... | collective-permute-start | bytes 2064392 | tf_op jit(solution)/shard_map/ppermute | solution.py:18
  23.0 11.6 %collective-permute-start.1 = (bf16[64,5376]{1,0:T(8,128)(2,1)S(1)}, bf16[64,5376]{1,0:T(8,128)(2,1)S(1)}, u32[]{:S(2)}, u32[]{:S(2)}) collective-permute-start(bf16[64,5376]{1,0:T(8,128)(2,1)S(1)} %collective-permute-done), channel_id=1, source_target_pairs={{0,1},{1,2},{2,3},{3,4},{4,5},{5,6},{6,7},{7,0},{8,9},{9,10},{10,1... | collective-permute-start | bytes 2064392 | tf_op jit(solution)/shard_map/ppermute | solution.py:18
  34.6 11.6 %collective-permute-start.2 = (bf16[64,5376]{1,0:T(8,128)(2,1)S(1)}, bf16[64,5376]{1,0:T(8,128)(2,1)S(1)}, u32[]{:S(2)}, u32[]{:S(2)}) collective-permute-start(bf16[64,5376]{1,0:T(8,128)(2,1)S(1)} %collective-permute-done.1), channel_id=1, source_target_pairs={{0,1},{1,2},{2,3},{3,4},{4,5},{5,6},{6,7},{7,0},{8,9},{9,10},{10,1... | collective-permute-start | bytes 2064392 | tf_op jit(solution)/shard_map/ppermute | solution.py:18
  46.2 11.6 %collective-permute-start.3 = (bf16[64,5376]{1,0:T(8,128)(2,1)S(1)}, bf16[64,5376]{1,0:T(8,128)(2,1)S(1)}, u32[]{:S(2)}, u32[]{:S(2)}) collective-permute-start(bf16[64,5376]{1,0:T(8,128)(2,1)S(1)} %collective-permute-done.2), channel_id=1, source_target_pairs={{0,1},{1,2},{2,3},{3,4},{4,5},{5,6},{6,7},{7,0},{8,9},{9,10},{10,1... | collective-permute-start | bytes 2064392 | tf_op jit(solution)/shard_map/ppermute | solution.py:18
  57.8 11.7 %collective-permute-start.4 = (bf16[64,5376]{1,0:T(8,128)(2,1)S(1)}, bf16[64,5376]{1,0:T(8,128)(2,1)}, u32[]{:S(2)}, u32[]{:S(2)}) collective-permute-start(bf16[64,5376]{1,0:T(8,128)(2,1)S(1)} %collective-permute-done.3), channel_id=1, source_target_pairs={{0,1},{1,2},{2,3},{3,4},{4,5},{5,6},{6,7},{7,0},{8,9},{9,10},{10,1... | collective-permute-start | bytes 2064392 | tf_op jit(solution)/shard_map/ppermute | solution.py:18
  69.4 11.9 %collective-permute-start.5 = (bf16[64,5376]{1,0:T(8,128)(2,1)}, bf16[64,5376]{1,0:T(8,128)(2,1)}, u32[]{:S(2)}, u32[]{:S(2)}) collective-permute-start(bf16[64,5376]{1,0:T(8,128)(2,1)} %collective-permute-done.4), channel_id=1, source_target_pairs={{0,1},{1,2},{2,3},{3,4},{4,5},{5,6},{6,7},{7,0},{8,9},{9,10},{10,1... | collective-permute-start | bytes 2064392 | tf_op jit(solution)/shard_map/ppermute | solution.py:18
  69.5 160.4 %reduce-scatter.2.cloned.1.call-start = ((), (), s32[]{:S(2)}) async-start(), calls=%async_computation.3 | async-start | bytes 6193152 | tf_op jit(solution)/shard_map/reduce_scatter | solution.py:152
  81.3 11.8 %collective-permute-start.6 = (bf16[64,5376]{1,0:T(8,128)(2,1)}, bf16[64,5376]{1,0:T(8,128)(2,1)S(1)}, u32[]{:S(2)}, u32[]{:S(2)}) collective-permute-start(bf16[64,5376]{1,0:T(8,128)(2,1)} %collective-permute-done.5), channel_id=1, source_target_pairs={{0,1},{1,2},{2,3},{3,4},{4,5},{5,6},{6,7},{7,0},{8,9},{9,10},{10,1... | collective-permute-start | bytes 2064392 | tf_op jit(solution)/shard_map/ppermute | solution.py:18
  112.4 14.6 %copy-start.8 = (f32[128]{0:T(128)S(1)}, f32[128]{0:T(128)}, u32[]{:S(2)}) copy-start(f32[128]{0:T(128)} %param.20) | copy-start | bytes 1540
  112.4 14.8 %copy-start.3 = (f32[512,64]{1,0:T(8,128)S(1)}, f32[512,64]{1,0:T(8,128)}, u32[]{:S(2)}) copy-start(f32[512,64]{1,0:T(8,128)} %copy.25) | copy-start | bytes 393220
  112.4 14.9 %copy-start.4 = (f32[512,64]{1,0:T(8,128)S(1)}, f32[512,64]{1,0:T(8,128)}, u32[]{:S(2)}) copy-start(f32[512,64]{1,0:T(8,128)} %copy.24) | copy-start | bytes 393220
  117.6 21.1 %copy-start.5 = (bf16[512,256]{1,0:T(8,128)(2,1)}, bf16[512,256]{1,0:T(8,128)(2,1)S(1)}, u32[]{:S(2)}) copy-start(bf16[512,256]{1,0:T(8,128)(2,1)S(1)} %fusion.23) | copy-start | bytes 786436
  117.6 21.3 %collective-permute-start.7 = (bf16[512,256]{1,0:T(8,128)(2,1)S(1)}, bf16[512,256]{1,0:T(8,128)(2,1)}, u32[]{:S(2)}, u32[]{:S(2)}) collective-permute-start(bf16[512,256]{1,0:T(8,128)(2,1)S(1)} %fusion.23), channel_id=1, source_target_pairs={{0,8},{8,16},{16,24},{24,32},{32,40},{40,48},{48,56},{56,64},{64,7... | collective-permute-start | bytes 786440 | tf_op jit(solution)/shard_map/ppermute | solution.py:45
  127.5 11.2 %copy-start.9 = (f32[128]{0:T(128)S(1)}, f32[128]{0:T(128)}, u32[]{:S(2)}) copy-start(f32[128]{0:T(128)} %param.19) | copy-start | bytes 1540
  128.4 13.7 %copy-start.1 = (f32[512,64]{0,1:T(8,128)S(1)}, f32[512,64]{0,1:T(8,128)}, u32[]{:S(2)}) copy-start(f32[512,64]{0,1:T(8,128)} %get-tuple-element.13) | copy-start | bytes 393220
  128.4 13.7 %copy-start.2 = (f32[512,64]{0,1:T(8,128)S(1)}, f32[512,64]{0,1:T(8,128)}, u32[]{:S(2)}) copy-start(f32[512,64]{0,1:T(8,128)} %get-tuple-element.14) | copy-start | bytes 393220
  128.4 16.4 %collective-permute-start.9 = (bf16[512,256]{1,0:T(8,128)(2,1)}, bf16[512,256]{1,0:T(8,128)(2,1)}, u32[]{:S(2)}, u32[]{:S(2)}) collective-permute-start(bf16[512,256]{1,0:T(8,128)(2,1)} %copy_bitcast_fusion), channel_id=1, source_target_pairs={{0,8},{8,16},{16,24},{24,32},{32,40},{40,48},{48,56},{56,64},{64,7... | collective-permute-start | bytes 786440 | tf_op jit(solution)/shard_map/ppermute | solution.py:45
  138.9 16.1 %collective-permute-start.8 = (bf16[512,256]{1,0:T(8,128)(2,1)}, bf16[512,256]{1,0:T(8,128)(2,1)}, u32[]{:S(2)}, u32[]{:S(2)}) collective-permute-start(bf16[512,256]{1,0:T(8,128)(2,1)} %collective-permute-done.7), channel_id=1, source_target_pairs={{0,8},{8,16},{16,24},{24,32},{32,40},{40,48},{48,56},{56,64},{64,7... | collective-permute-start | bytes 786440 | tf_op jit(solution)/shard_map/ppermute | solution.py:45
  144.8 18.6 %collective-permute-start.10 = (bf16[512,256]{1,0:T(8,128)(2,1)}, bf16[512,256]{1,0:T(8,128)(2,1)}, u32[]{:S(2)}, u32[]{:S(2)}) collective-permute-start(bf16[512,256]{1,0:T(8,128)(2,1)} %collective-permute-done.9), channel_id=1, source_target_pairs={{0,8},{8,16},{16,24},{24,32},{32,40},{40,48},{48,56},{56,64},{64,7... | collective-permute-start | bytes 786440 | tf_op jit(solution)/shard_map/ppermute | solution.py:45
  180.8 50.4 %copy-start.7 = (f32[5376]{0:T(1024)S(1)}, f32[5376]{0:T(1024)}, u32[]{:S(2)}) copy-start(f32[5376]{0:T(1024)} %param.23) | copy-start | bytes 64516
Sparse Core Ops, SparseCore 0:
  9.5 85.2 all-gather.2
  96.9 72.9 all-gather.4
  188.5 41.3 reduce-scatter.1
